TPU v7x, 64 devices: a 2x2x8 block of a 4x4x8 slice. The times are simulated.
64 devices in a mesh: data: 4 (over x, y), model: 16 (over z, core).
Axes of the slice: x: 2, y: 2, z: 8, core: 2. Of those that a mesh axis runs over, the one named last changes fastest.
The devices are a block of a 4x4x8 slice.
Arguments:
- queries: bfloat16 [256, 1536], P('data'), parts along dimension 0
- w_head: bfloat16 [1536, 151936], P(None, 'model')
- ds_keys: bfloat16 [262144, 1536], P('model')
- ds_tokens: int32 [262144], P('model')
- temperature: float32 [1], replicated
- mix_weight: float32 [1], replicated
Outputs:
- output: float32 [256, 151936], P('data', 'model'), parts along dimension 0
There are 4 independent parts. A program takes and returns all parts, laid end to end along the dimension named above; an argument that names none is the same for every part.
All inputs are finite; a program needn't handle non-finite values.
Results may differ from a plain program's by a relative error of at most 0.001.
Values are sent between devices in bfloat16 or wider.
A program may use at most 768 MiB of HBM per device.

v0:
```python
import jax
import jax.numpy as jnp
from jax import lax
from jax.sharding import PartitionSpec as P


def solution(mesh):
    group_size = mesh.shape["model"]

    def local_step(queries, w_shard, key_shard, tok_shard, value_a11, mix_weight):
        row_count = queries.shape[0]
        vocab_size = w_shard.shape[1] * group_size
        cross_dot = jnp.einsum("bd,nd->bn", queries, key_shard, preferred_element_type=jnp.float32)
        key_sq = jnp.sum(jnp.square(key_shard.astype(jnp.float32)), axis=1)
        scores = (2.0 * cross_dot - key_sq[None, :]) / value_a11[0]
        row_max = lax.pmax(jnp.max(scores, axis=1), "model")
        weights = jnp.exp(scores - row_max[:, None])
        row_total = lax.psum(jnp.sum(weights, axis=1), "model")
        local_hist = jnp.zeros((row_count, vocab_size), jnp.float32).at[:, tok_shard].add(weights)
        histogram = lax.psum_scatter(local_hist, "model", scatter_dimension=1, tiled=True)
        logits = jnp.dot(queries, w_shard, preferred_element_type=jnp.float32)
        lm_max = lax.pmax(jnp.max(logits, axis=1), "model")
        lm_exp = jnp.exp(logits - lm_max[:, None])
        lm_total = lax.psum(jnp.sum(lm_exp, axis=1), "model")
        mix_value = mix_weight[0]
        p_knn = histogram / row_total[:, None]
        p_lm = lm_exp / lm_total[:, None]
        return jnp.log(mix_value * p_knn + (1.0 - mix_value) * p_lm)

    return jax.shard_map(
        local_step,
        mesh=mesh,
        in_specs=(P("data", None), P(None, "model"), P("model", None), P("model"), P(), P()),
        out_specs=P("data", "model"),
        check_vma=False,
    )
```

profile of v0, /device:TPU:21, one launch (start us, length us, event | category | flops | bytes accessed | tf_op | source)
XLA Modules:
  0.0 806.4 jit_solution(17869406816527453332)
XLA Ops:
  6.5 0.0 copy-start
  6.6 0.0 all-reduce.5.cloned.1.call-start
  6.6 0.9 compare_select_fusion
  8.1 16.5 %multiply_reduce_fusion = f32[16384]{0:T(1024)S(1)} fusion(bf16[16384,1536]{1,0:T(8,128)(2,1)} %param.8), kind=kLoop, calls=%fused_computation.2 | loop fusion | flops 75481088 | bytes 50397184 | tf_op jit(solution)/shard_map/reduce_sum | solution.py:14
  24.6 0.0 copy-done
  24.6 14.6 %fusion.15 = (f32[64]{0:T(128)S(1)}, f32[64,9496]{1,0:T(8,128)S(1)}) fusion(bf16[64,1536]{1,0:T(8,128)(2,1)S(1)} %copy-done, bf16[1536,9496]{0,1:T(8,128)(2,1)} %param.7), kind=kOutput, calls=%fused_computation.21 | convolution fusion | flops 1867597312 | bytes 31799552 | tf_op jit(solution)/shard_map/dot_general | solution.py:21
  39.2 23.7 %fusion.14 = (f32[64]{0:T(128)S(1)}, f32[64,16384]{1,0:T(8,128)}) fusion(f32[]{:T(128)} %bitcast.11, f32[16384]{0:T(1024)S(1)} %multiply_reduce_fusion, bf16[64,1536]{1,0:T(8,128)(2,1)S(1)} %copy-done, bf16[16384,1536]{1,0:T(8,128)(2,1)} %param.8), kind=kOutput, calls=%fused_computation.20 | convolution fusion | flops 3225419776 | bytes 54788356 | tf_op jit(solution)/shard_map/bd,nd->bn/dot_general | solution.py:13
  62.9 29.0 %all-reduce.2 = (f32[64]{0:T(128)S(1)}, f32[64]{0:T(128)S(1)}) all-reduce(f32[64]{0:T(128)S(1)} %get-tuple-element.13, f32[64]{0:T(128)S(1)} %get-tuple-element.15), channel_id=1, replica_groups=mesh['data'=4,'model'=16] {'model'}, use_global_device_ids=true, to_apply=%region_2.0 | all-reduce | flops 128 | bytes 1024 | tf_op jit(solution)/shard_map/pmax | solution.py:16
  91.9 4.8 fusion.8
  96.7 6.9 copy.9
  103.6 7.1 sort
  110.8 212.5 %scatter_custom_fusion = f32[64,151936]{0,1:T(8,128)} fusion(s32[16384]{0:T(1024)S(1)} %get-tuple-element.5, f32[]{:T(128)} %constant.6.clone.1, f32[16384,64]{1,0:T(8,128)} %copy.9, s32[16384]{0:T(1024)S(1)} %broadcast_clamp_fusion), kind=kCustom, calls=%fused_computation.3 | custom fusion | flops 1048576 | bytes 38896128 | tf_op jit(solution)/shard_map/scatter-add | solution.py:19
  323.2 56.7 %copy.10 = f32[64,151936]{1,0:T(8,128)} copy(f32[64,151936]{0,1:T(8,128)} %scatter_custom_fusion) | data formatting | bytes 77791232 | tf_op jit(solution)/shard_map/scatter-add | solution.py:19
  380.0 0.0 copy-start.2
  380.0 0.1 all-reduce.5.cloned.1.call-update
  380.7 0.0 copy-done.2
  380.7 0.6 dynamic-slice
  381.9 0.0 copy-start.1
  382.0 0.6 fusion.13
  382.5 26.2 %all-reduce.1 = (f32[64]{0:T(128)S(1)}, f32[64]{0:T(128)S(1)}) all-reduce(f32[64]{0:T(128)S(1)} %fusion.13, f32[64]{0:T(128)S(1)} %get-tuple-element.11), channel_id=1, replica_groups=mesh['data'=4,'model'=16] {'model'}, use_global_device_ids=true, to_apply=%region_10.0 | all-reduce | flops 128 | bytes 1024 | tf_op jit(solution)/shard_map/psum | solution.py:24
  408.7 386.7 %all-reduce.5.cloned.1.call-done = f32[64,151936]{1,0:T(8,128)} async-done(((f32[64,151936]{1,0:T(8,128)}), f32[64,151936]{1,0:T(8,128)}) %all-reduce.5.cloned.1.call-update) | async-done | bytes 38895632
  795.4 4.1 fusion.12
  799.5 0.0 copy-done.1
  (2 shorter events, 0.0 us)
Async XLA Ops:
  6.5 18.1 %copy-start = (bf16[64,1536]{1,0:T(8,128)(2,1)S(1)}, bf16[64,1536]{1,0:T(8,128)(2,1)}, u32[]{:S(2)}) copy-start(bf16[64,1536]{1,0:T(8,128)(2,1)} %param.6) | copy-start | bytes 589828
  6.6 788.9 %all-reduce.5.cloned.1.call-start = ((), (), s32[]{:S(2)}) async-start(), calls=%async_computation | async-start | bytes 77791232
  380.0 0.7 copy-start.2
  381.9 417.6 %copy-start.1 = (bf16[64,1536]{1,0:T(8,128)(2,1)S(1)}, bf16[64,1536]{1,0:T(8,128)(2,1)}, u32[]{:S(2)}) copy-start(bf16[64,1536]{1,0:T(8,128)(2,1)} %param.6) | copy-start | bytes 589828
Sparse Core Ops, SparseCore 0:
  380.2 415.1 all-reduce.4
where the time goes:
time: 808 us; the launch traced here: 806 us
  waiting for transfers between devices  387 us (48%)
  other arithmetic  247 us (31%)
  local copies, waits for them, and re-layouts  64.2 us (8%)
  blocking collectives  55.1 us (7%)
  matrix products  38.3 us (5%)
  between operations  15.4 us (2%)
    unnamed x2, waiting for transfers between devices  387 us
    scatter-add x3, other arithmetic, local_step(): jnp.zeros((row_count, vocab_size), jnp.float32).at[:, tok_shard]  220 us
    scatter-add x2, local copies, waits for them, and re-layouts, local_step(): jnp.zeros((row_count, vocab_size), jnp.float32).at[:, tok_shard]  56.8 us
    pmax x1, blocking collectives, local_step(): row_max = lax.pmax(jnp.max(scores, axis=1), 'model')  29 us
    psum x1, blocking collectives, local_step(): lm_total = lax.psum(jnp.sum(lm_exp, axis=1), 'model')  26.2 us
    dot_general x1, matrix products, local_step(): jnp.einsum('bd,nd->bn', queries, key_shard, preferred_element_type=jnp.fl...  23.7 us
    reduce_sum x1, other arithmetic, local_step(): key_sq = jnp.sum(jnp.square(key_shard.astype(jnp.float32)), axis=1)  16.5 us
  transfers between devices with their start and end apart: 1, of which 1 were waited for; matrix products, arithmetic and copies ran while one was open for 0% of the time, Pallas kernels for 0%

commit v1 on v0

v1 whole, which is shorter than its diff:
```python
import functools
import math

import jax
import jax.numpy as jnp
from jax import lax
from jax.experimental import pallas as pl
from jax.experimental.pallas import tpu as pltpu
from jax.sharding import PartitionSpec as P

MESH = pl.DeviceIdType.MESH
LANES = 128
KEY_TILE = 512
KEY_BUFS = 4
HEAD_TILE = 512
HEAD_BUFS = 3
VMEM_LIMIT = 60 * 1024 * 1024


def round_up(value, step):
    return (value + step - 1) // step * step


def slot_kernel(group, vocab, rows, starts_ref, tok_ref, ord_ref, col_ref, idx_ref):
    lane = lax.broadcasted_iota(jnp.int32, (rows, LANES), 1)
    slot = lax.broadcasted_iota(jnp.int32, (rows, LANES), 0) * LANES + lane
    for d in range(group):
        start = starts_ref[d]
        count = starts_ref[d + 1] - start
        row, off = start // LANES, lax.rem(start, LANES)
        shift = lax.rem(LANES - off, LANES)

        def shifted(ref):
            low = pltpu.roll(ref[pl.ds(row, rows), :], shift, 1)
            high = pltpu.roll(ref[pl.ds(row + 1, rows), :], shift, 1)
            return jnp.where(lane < LANES - off, low, high)

        used = slot < count
        col_ref[d] = jnp.where(used, shifted(tok_ref) - d * vocab, vocab)
        idx_ref[d] = jnp.where(used, shifted(ord_ref), 0)


def exchange_kernel(
    group, half, idx_ref, temp_ref, over_ref, query_ref, col_ref, key_hbm, head_hbm,
    recv_hbm, rcol_hbm, rstat_hbm, logit_ref,
    key_buf, head_buf, score, send, stat, key_sem, head_sem,
    data_send, data_recv, col_send, col_recv, stat_send, stat_recv, own_sem,
):
    me = lax.axis_index("model")
    n_local, vocab = key_hbm.shape[0], head_hbm.shape[0]
    slots = idx_ref.shape[0] // group

    barrier = pltpu.get_barrier_semaphore()
    for k in range(1, group):
        pl.semaphore_signal(
            barrier, inc=1, device_id={"model": lax.rem(me + k, group)}, device_id_type=MESH
        )

    def key_copy(step):
        return pltpu.make_async_copy(
            key_hbm.at[pl.ds(step * KEY_TILE, KEY_TILE), :],
            key_buf.at[lax.rem(step, KEY_BUFS)],
            key_sem.at[lax.rem(step, KEY_BUFS)],
        )

    head_full = vocab // HEAD_TILE
    head_rest = vocab - head_full * HEAD_TILE

    def head_copy(step):
        return pltpu.make_async_copy(
            head_hbm.at[pl.ds(step * HEAD_TILE, HEAD_TILE), :],
            head_buf.at[lax.rem(step, HEAD_BUFS)],
            head_sem.at[lax.rem(step, HEAD_BUFS)],
        )

    key_steps = n_local // KEY_TILE
    for step in range(KEY_BUFS - 1):
        key_copy(step).start()

    temp = temp_ref[0]

    def merge(total, tile):
        top, acc = total
        new = jnp.maximum(top, jnp.max(tile, axis=0, keepdims=True))
        acc = acc * jnp.exp(top - new) + jnp.sum(jnp.exp(tile - new), axis=0, keepdims=True)
        return new, acc

    empty = (jnp.full((1, LANES), -3e38, jnp.float32), jnp.zeros((1, LANES), jnp.float32))

    def score_step(step, total):
        @pl.when(step + KEY_BUFS - 1 < key_steps)
        def _():
            key_copy(step + KEY_BUFS - 1).start()

        key_copy(step).wait()
        keys = key_buf[lax.rem(step, KEY_BUFS)]
        cross = jnp.dot(keys, query_ref[...], preferred_element_type=jnp.float32)
        wide = keys.astype(jnp.float32)
        square = jnp.sum(wide * wide, axis=1, keepdims=True)
        tile = (2.0 * cross - square) / temp
        score[pl.ds(pl.multiple_of(step * KEY_TILE, KEY_TILE), KEY_TILE), :] = tile
        return merge(total, tile)

    knn_max, knn_sum = lax.fori_loop(0, key_steps, score_step, empty)

    for step in range(HEAD_BUFS - 1):
        head_copy(step).start()

    pl.semaphore_wait(barrier, group - 1)

    left = lax.broadcasted_iota(jnp.int32, (1, LANES), 1) < LANES // 2

    def pack(k, slot):
        base = lax.rem(me + k, group) * slots

        def rows(t, carry):
            for i in range(8):
                j = t * 8 + i
                a = idx_ref[base + j]
                b = idx_ref[base + half + j]
                row = jnp.where(left, score[pl.ds(a, 1), :], score[pl.ds(b, 1), :])
                send[slot, pl.ds(j, 1), :] = row
            return carry

        lax.fori_loop(0, half // 8, rows, 0)

    def data_copy(k):
        return pltpu.make_async_remote_copy(
            src_ref=send.at[k], dst_ref=recv_hbm.at[me],
            send_sem=data_send.at[k], recv_sem=data_recv.at[k],
            device_id={"model": lax.rem(me + k, group)}, device_id_type=MESH,
        )

    def cols_copy(k):
        return pltpu.make_async_remote_copy(
            src_ref=col_ref.at[lax.rem(me + k, group)], dst_ref=rcol_hbm.at[me],
            send_sem=col_send.at[k], recv_sem=col_recv.at[k],
            device_id={"model": lax.rem(me + k, group)}, device_id_type=MESH,
        )

    def stat_copy(k):
        return pltpu.make_async_remote_copy(
            src_ref=stat, dst_ref=rstat_hbm.at[me],
            send_sem=stat_send.at[k], recv_sem=stat_recv.at[k],
            device_id={"model": lax.rem(me + k, group)}, device_id_type=MESH,
        )

    mid = group // 2
    order = []
    for k in range(1, mid):
        order += [mid - k, mid + k] if k % 2 else [mid + k, mid - k]
    order = [mid] + order
    waiting = None
    for k in order:
        pack(k, k)
        if waiting is not None:
            data_copy(waiting).start()
        waiting = k
    pack(0, 0)
    data_copy(waiting).start()
    for k in order:
        cols_copy(k).start()

    def head_tile(rows_ref, where):
        tile = jnp.dot(rows_ref, query_ref[...], preferred_element_type=jnp.float32)
        logit_ref[where, :] = tile
        return tile

    rest_copy = pltpu.make_async_copy(
        head_hbm.at[pl.ds(head_full * HEAD_TILE, head_rest), :],
        head_buf.at[HEAD_BUFS, pl.ds(0, head_rest), :],
        head_sem.at[HEAD_BUFS],
    )
    if head_rest:
        rest_copy.start()

    def head_step(step, total):
        @pl.when(step + HEAD_BUFS - 1 < head_full)
        def _():
            head_copy(step + HEAD_BUFS - 1).start()

        head_copy(step).wait()
        where = pl.ds(pl.multiple_of(step * HEAD_TILE, HEAD_TILE), HEAD_TILE)
        return merge(total, head_tile(head_buf[lax.rem(step, HEAD_BUFS)], where))

    total = lax.fori_loop(0, head_full, head_step, empty)
    if head_rest:
        rest_copy.wait()
        where = pl.ds(head_full * HEAD_TILE, head_rest)
        total = merge(total, head_tile(head_buf[HEAD_BUFS, :head_rest, :], where))
    lm_max, lm_sum = total

    stat[0:1, :] = knn_max
    stat[1:2, :] = knn_sum
    stat[2:3, :] = lm_max
    stat[3:4, :] = lm_sum
    stat[4:8, :] = jnp.full((4, LANES), over_ref[0], jnp.float32)

    own = [
        pltpu.make_async_copy(send.at[0], recv_hbm.at[me], own_sem.at[0]),
        pltpu.make_async_copy(col_ref.at[me], rcol_hbm.at[me], own_sem.at[1]),
        pltpu.make_async_copy(stat, rstat_hbm.at[me], own_sem.at[2]),
    ]
    for copy in own:
        copy.start()
    for k in order:
        stat_copy(k).start()
    for copy in own:
        copy.wait()
    for k in order:
        stat_copy(k).wait()
        cols_copy(k).wait()
        data_copy(k).wait()


def finish_kernel(
    group, half, slots, col_ref, mix_ref, recv_ref, stat_ref, logit_ref, out_ref, sum_ref,
    weight, hist_a, hist_b, hist_c, hist_d,
):
    vocab = logit_ref.shape[0]
    hists = (hist_a, hist_b, hist_c, hist_d)

    def clear(i, carry):
        where = pl.ds(pl.multiple_of(i * 8, 8), 8)
        for hist in hists:
            hist[where, :] = jnp.zeros((8, LANES), jnp.float32)
        return carry

    lax.fori_loop(0, hist_a.shape[0] // 8, clear, 0)

    def combine(top_row):
        top = stat_ref[0, top_row : top_row + 1, :]
        for d in range(1, group):
            top = jnp.maximum(top, stat_ref[d, top_row : top_row + 1, :])
        acc = jnp.zeros((1, LANES), jnp.float32)
        for d in range(group):
            acc = acc + stat_ref[d, top_row + 1 : top_row + 2, :] * jnp.exp(
                stat_ref[d, top_row : top_row + 1, :] - top
            )
        return top, acc

    knn_max, knn_sum = combine(0)
    lm_max, lm_sum = combine(2)
    over = stat_ref[0, 4:5, :]
    for d in range(1, group):
        over = jnp.maximum(over, stat_ref[d, 4:5, :])
    sum_ref[0:1, :] = knn_max
    sum_ref[1:2, :] = knn_sum
    sum_ref[2:3, :] = lm_max
    sum_ref[3:4, :] = lm_sum
    sum_ref[4:8, :] = jnp.broadcast_to(over, (4, LANES))

    for d in range(group):

        def to_weight(i, carry):
            src = pl.ds(pl.multiple_of(i * 8, 8), 8)
            dst = pl.ds(pl.multiple_of(d * half + i * 8, 8), 8)
            weight[dst, :] = jnp.exp(recv_ref[d, src, :] - knn_max)
            return carry

        lax.fori_loop(0, half // 8, to_weight, 0)

    def add_rows(t, carry):
        d = t // (half // 8)
        j = (t - d * (half // 8)) * 8
        base = d * slots + j
        for i in range(8):
            row = weight[pl.ds(t * 8 + i, 1), :]
            low, high = hists[2 * (i % 2)], hists[2 * (i % 2) + 1]
            a = col_ref[base + i]
            low[pl.ds(a, 1), :] = low[pl.ds(a, 1), :] + row
            b = col_ref[base + half + i]
            high[pl.ds(b, 1), :] = high[pl.ds(b, 1), :] + row
        return carry

    lax.fori_loop(0, group * (half // 8), add_rows, 0)

    mix = mix_ref[0]
    knn_scale = mix / knn_sum
    lm_scale = (1.0 - mix) / lm_sum

    def tile(start, rows):
        where = pl.ds(start, rows)
        high = hist_b[where, :] + hist_d[where, :]
        hist = hist_a[where, :] + hist_c[where, :] + pltpu.roll(high, LANES // 2, 1)
        prob = hist * knn_scale + jnp.exp(logit_ref[where, :] - lm_max) * lm_scale
        return jnp.log(prob)

    full = vocab // LANES

    def write(i, carry):
        start = pl.multiple_of(i * LANES, LANES)
        out_ref[:, pl.ds(start, LANES)] = tile(start, LANES).T[: LANES // 2, :]
        return carry

    lax.fori_loop(0, full, write, 0)
    rest = vocab - full * LANES
    if rest:
        last = jnp.concatenate(
            [tile(full * LANES, rest), jnp.zeros((LANES - rest, LANES), jnp.float32)], axis=0
        )
        out_ref[:, full * LANES :] = last.T[: LANES // 2, :rest]


def solution(mesh):
    group = mesh.shape["model"]

    def local_step(queries, w_shard, key_shard, tok_shard, temperature, mix_weight):
        row_count, depth = queries.shape
        vocab, n_local = w_shard.shape[1], key_shard.shape[0]
        mean = n_local / group
        cap = round_up(int(mean + 4.5 * math.sqrt(mean)), 16)
        half = cap // 2
        slot_rows = round_up(cap, LANES) // LANES
        slots = slot_rows * LANES

        order_tok, order_idx = lax.sort(
            (tok_shard, lax.iota(jnp.int32, n_local)), num_keys=1, is_stable=False
        )
        bounds = jnp.arange(group + 1, dtype=jnp.int32) * vocab
        starts = jnp.sum(
            (tok_shard[None, :] < bounds[:, None]).astype(jnp.int32), axis=1
        )
        over = (jnp.max(starts[1:] - starts[:-1]) > cap).astype(jnp.float32).reshape(1)
        pad = (slot_rows + 8) * LANES
        fill = jnp.zeros((pad,), jnp.int32)
        shape_2d = ((n_local + pad) // LANES, LANES)
        tok_2d = jnp.concatenate([order_tok, fill]).reshape(shape_2d)
        idx_2d = jnp.concatenate([order_idx, fill]).reshape(shape_2d)

        smem = pl.BlockSpec(memory_space=pltpu.SMEM)
        vmem = pl.BlockSpec(memory_space=pltpu.VMEM)
        hbm = pl.BlockSpec(memory_space=pl.ANY)
        table = jax.ShapeDtypeStruct((group, slot_rows, LANES), jnp.int32)
        cols, idx = pl.pallas_call(
            functools.partial(slot_kernel, group, vocab, slot_rows),
            out_shape=(table, table),
            in_specs=[smem, vmem, vmem],
            out_specs=(vmem, vmem),
            name="slots",
        )(starts, tok_2d, idx_2d)

        query_t = jnp.concatenate([queries, queries], axis=0).T
        recv, rcols, rstat, logits = pl.pallas_call(
            functools.partial(exchange_kernel, group, half),
            out_shape=(
                jax.ShapeDtypeStruct((group, half, LANES), jnp.float32),
                table,
                jax.ShapeDtypeStruct((group, 8, LANES), jnp.float32),
                jax.ShapeDtypeStruct((vocab, LANES), jnp.float32),
            ),
            in_specs=[smem, smem, smem, vmem, vmem, hbm, hbm],
            out_specs=(hbm, hbm, hbm, vmem),
            scratch_shapes=[
                pltpu.VMEM((KEY_BUFS, KEY_TILE, depth), jnp.bfloat16),
                pltpu.VMEM((HEAD_BUFS + 1, HEAD_TILE, depth), jnp.bfloat16),
                pltpu.VMEM((n_local, LANES), jnp.float32),
                pltpu.VMEM((group, half, LANES), jnp.float32),
                pltpu.VMEM((8, LANES), jnp.float32),
                pltpu.SemaphoreType.DMA((KEY_BUFS,)),
                pltpu.SemaphoreType.DMA((HEAD_BUFS + 1,)),
                pltpu.SemaphoreType.DMA((group,)),
                pltpu.SemaphoreType.DMA((group,)),
                pltpu.SemaphoreType.DMA((group,)),
                pltpu.SemaphoreType.DMA((group,)),
                pltpu.SemaphoreType.DMA((group,)),
                pltpu.SemaphoreType.DMA((group,)),
                pltpu.SemaphoreType.DMA((3,)),
            ],
            compiler_params=pltpu.CompilerParams(
                collective_id=0, has_side_effects=True, vmem_limit_bytes=VMEM_LIMIT
            ),
            name="exchange",
        )(idx.reshape(-1), temperature, over, query_t, cols, key_shard, w_shard.T)

        hist_shape = pltpu.VMEM((round_up(vocab + 1, 8), LANES), jnp.float32)
        fast, sums = pl.pallas_call(
            functools.partial(finish_kernel, group, half, slots),
            out_shape=(
                jax.ShapeDtypeStruct((row_count, vocab), jnp.float32),
                jax.ShapeDtypeStruct((8, LANES), jnp.float32),
            ),
            in_specs=[smem, smem, vmem, vmem, vmem],
            out_specs=(vmem, vmem),
            scratch_shapes=[pltpu.VMEM((group * half, LANES), jnp.float32)] + [hist_shape] * 4,
            compiler_params=pltpu.CompilerParams(vmem_limit_bytes=VMEM_LIMIT),
            name="finish",
        )(rcols.reshape(-1), mix_weight, recv, rstat, logits)

        def dense(unused):
            me = lax.axis_index("model")
            row_max, row_total = sums[0, :row_count], sums[1, :row_count]
            lm_max, lm_total = sums[2, :row_count], sums[3, :row_count]
            cross_dot = jnp.einsum("bd,nd->nb", queries, key_shard, preferred_element_type=jnp.float32)
            key_sq = jnp.sum(jnp.square(key_shard.astype(jnp.float32)), axis=1)
            scores = (2.0 * cross_dot - key_sq[:, None]) / temperature[0]
            weights = jnp.exp(scores - row_max[None, :])
            ring = [(i, (i + 1) % group) for i in range(group)]

            def turn(k, acc):
                acc = lax.ppermute(acc, "model", ring)
                col = tok_shard - lax.rem(me + group - 1 - k, group) * vocab
                col = jnp.where((col >= 0) & (col < vocab), col, vocab)
                return acc.at[col].add(weights)

            acc = jnp.zeros((vocab + 1, row_count), jnp.float32)
            acc = lax.fori_loop(0, group, turn, acc)
            logit = jnp.dot(queries, w_shard, preferred_element_type=jnp.float32)
            p_lm = jnp.exp(logit - lm_max[:, None]) / lm_total[:, None]
            p_knn = acc[:vocab].T / row_total[:, None]
            mix_value = mix_weight[0]
            return jnp.log(mix_value * p_knn + (1.0 - mix_value) * p_lm)

        return lax.cond(sums[4, 0] > 0.0, dense, lambda kept: kept, fast)

    return jax.shard_map(
        local_step,
        mesh=mesh,
        in_specs=(P("data", None), P(None, "model"), P("model", None), P("model"), P(), P()),
        out_specs=P("data", "model"),
        check_vma=False,
    )
```

time: 808 us -> 251 us (0.31)
  waiting for transfers between devices: 387 us -> 0 us
  other arithmetic: 247 us -> 11.4 us
  Pallas kernels: 0 us -> 231 us
  local copies, waits for them, and re-layouts: 64.2 us -> 5.42 us
  blocking collectives: 55.1 us -> 0 us
  matrix products: 38.3 us -> 0 us
  between operations: 15.4 us -> 2.73 us
    unnamed x2 -> x0, waiting for transfers between devices: 387 us -> none
    pallas_call x0 -> x3, Pallas kernels: none -> 231 us  [the longest x1 153 us: local_step(): pl.pallas_call(functools.partial(exchange_kernel, group, half), out_shape...]
    scatter-add x3 -> x0, other arithmetic: 220 us -> none  [local_step(): jnp.zeros((row_count, vocab_size), jnp.float32).at[:, tok_shard]]
    scatter-add x2 -> x0, local copies, waits for them, and re-layouts: 56.8 us -> none  [local_step(): jnp.zeros((row_count, vocab_size), jnp.float32).at[:, tok_shard]]
    dot_general x2 -> x0, matrix products: 38.3 us -> none  [the longest x1 23.7 us: local_step(): jnp.einsum('bd,nd->bn', queries, key_shard, preferred_element_type=jnp.fl...]
    pmax x1 -> x0, blocking collectives: 29 us -> none  [local_step(): row_max = lax.pmax(jnp.max(scores, axis=1), 'model')]
    psum x1 -> x0, blocking collectives: 26.2 us -> none  [local_step(): lm_total = lax.psum(jnp.sum(lm_exp, axis=1), 'model')]
    reduce_sum x3 -> x1, other arithmetic: 21.9 us -> 1.73 us  [local_step(): jnp.sum((tok_shard[None, :] < bounds[:, None]).astype(jnp.int32), axis=1)]
  transfers between devices with their start and end apart: 1 -> 0, of which waited for: 1 -> 0; matrix products, arithmetic and copies ran while one was open for 0% -> 0% of each run, Pallas kernels for 0% -> 0%
where the time goes in v1:
time: 251 us
  Pallas kernels  231 us (92%)
  other arithmetic  11.4 us (5%)
  local copies, waits for them, and re-layouts  5.42 us (2%)
  between operations  2.73 us (1%)
    pallas_call x1, Pallas kernels, local_step(): pl.pallas_call(functools.partial(exchange_kernel, group, half), out_shape...  153 us
    pallas_call x1, Pallas kernels, local_step(): pl.pallas_call(functools.partial(finish_kernel, group, half, slots), out_...  76.2 us
    sort x1, other arithmetic, local_step(): lax.sort((tok_shard, lax.iota(jnp.int32, n_local)), num_keys=1, is_stable...  7.28 us

profile of v1, /device:TPU:21, one launch (start us, length us, event | category | flops | bytes accessed | tf_op | source)
XLA Modules:
  0.0 250.7 jit_solution(14241129564418708637)
XLA Ops:
  0.0 7.3 %sort.15 = (s32[16384]{0:T(1024)S(1)}, s32[16384]{0:T(1024)S(1)}) sort(s32[16384]{0:T(1024)} %param.13, s32[16384]{0:T(1024)S(1)} %iota.9), dimensions={0}, to_apply=%region_1.0 | sort | flops 229376 | bytes 262144 | tf_op jit(solution)/shard_map/sort | solution.py:317
  7.3 0.7 pad_bitcast_fusion
  8.0 1.7 convert_reduce_fusion.starts_ref
  9.7 1.8 slots.1
  11.5 1.5 reshape.66.idx_ref
  13.1 1.4 subtract_reduce_fusion
  15.1 1.1 copy.33
  16.3 1.0 maximum_bitcast_fusion.query_ref
  17.9 152.9 %exchange.1 = (f32[16,584,128]{2,1,0:T(8,128)}, s32[16,10,128]{2,1,0:T(8,128)}, f32[16,8,128]{2,1,0:T(8,128)}, f32[9496,128]{1,0:T(8,128)}) custom-call(s32[20480]{0:T(1024)} %reshape.66.idx_ref, f32[1]{0:T(128)S(6)} %copy.50.temp_ref, f32[1]{0:T(128)} %bitcast.11.over_ref, bf16[1536,128]{1,0:T(8,128)(2,1)} %maximum_bitcast_fusion.query_ref, ...), custom_call_target="tpu_custom_call" | custom-call | tf_op jit(solution)/shard_map/exchange/pallas_call | solution.py:344
  170.8 1.5 reshape.69.col_ref
  173.0 0.0 copy-start.1
  173.0 76.2 %finish.1 = (f32[64,9496]{1,0:T(8,128)}, f32[8,128]{1,0:T(8,128)S(1)}) custom-call(s32[20480]{0:T(1024)} %reshape.69.col_ref, f32[1]{0:T(128)S(6)} %copy.51.mix_ref, f32[16,584,128]{2,1,0:T(8,128)} %get-tuple-element.175.recv_ref, f32[16,8,128]{2,1,0:T(8,128)} %get-tuple-element.176.stat_ref, f32[9496,128]{1,0:T(8,128)} %get-tuple-element.177.logit_ref), custom_call_target="tpu_custom_call" | custom-call | tf_op jit(solution)/shard_map/finish/pallas_call | solution.py:377
  249.2 0.5 slice.26
  250.3 0.0 copy-done.1
  250.3 0.2 conditional.1
  (2 shorter events, 0.0 us)
Async XLA Ops:
  173.0 77.3 %copy-start.1 = (bf16[64,1536]{1,0:T(8,128)(2,1)S(1)}, bf16[64,1536]{1,0:T(8,128)(2,1)}, u32[]{:S(2)}) copy-start(bf16[64,1536]{1,0:T(8,128)(2,1)} %param.10) | copy-start | bytes 589828

commit v2 on v1

v2 whole, which is shorter than its diff:
```python
import functools
import math

import jax
import jax.numpy as jnp
from jax import lax
from jax.experimental import pallas as pl
from jax.experimental.pallas import tpu as pltpu
from jax.sharding import PartitionSpec as P

MESH = pl.DeviceIdType.MESH
LANES = 128
KEY_TILE = 512
KEY_BUFS = 4
HEAD_TILE = 512
HEAD_BUFS = 3
COLS = 256
WINDOW = 64
BATCH = 4
VMEM_LIMIT = 60 * 1024 * 1024


def round_up(value, step):
    return (value + step - 1) // step * step


def slot_kernel(group, vocab, cap, rows, n_local, tok_ref, ord_ref, col_ref, idx_ref, off_ref, over_ref):
    lane = lax.broadcasted_iota(jnp.int32, (rows, LANES), 1)
    slot = lax.broadcasted_iota(jnp.int32, (rows, LANES), 0) * LANES + lane
    bound = lax.broadcasted_iota(jnp.int32, (LANES, LANES), 0)
    across = lax.broadcasted_iota(jnp.int32, (LANES, LANES), 1)
    tokens = tok_ref[: n_local // LANES, :]

    def below(limit):
        return jnp.sum((tokens < limit).astype(jnp.int32))

    starts = [0] + [below(d * vocab) for d in range(1, group)] + [n_local]
    table = jnp.zeros((LANES, LANES), jnp.float32)
    most = jnp.int32(0)
    for d in range(group):
        start, count = starts[d], starts[d + 1] - starts[d]
        most = jnp.maximum(most, count)
        row, off = start // LANES, start % LANES
        shift = (LANES - off) % LANES

        def shifted(ref):
            low = pltpu.roll(ref[pl.ds(row, rows), :], shift, 1)
            high = pltpu.roll(ref[pl.ds(row + 1, rows), :], shift, 1)
            return jnp.where(lane < LANES - off, low, high)

        used = slot < count
        col = jnp.where(used, shifted(tok_ref) - d * vocab, vocab)
        col_ref[d] = col
        idx_ref[d * rows : (d + 1) * rows, :] = jnp.where(used, shifted(ord_ref), 0)
        first = jnp.where(used, col // COLS, LANES)
        hits = jnp.zeros((LANES, LANES), jnp.float32)
        for r in range(rows):
            hits = hits + jnp.where(first[r : r + 1, :] < bound, 1.0, 0.0)
        table = jnp.where(across == d, jnp.sum(hits, axis=1, keepdims=True), table)
    widest = jnp.max(table[1:, :] - table[:-1, :])
    over = jnp.where((most > cap) | (widest > WINDOW), 1.0, 0.0)
    over_ref[...] = jnp.full((8, LANES), over, jnp.float32)
    turned = jnp.minimum(table, float(cap)).T.astype(jnp.int32)
    for d in range(group):
        off_ref[d] = turned[d : d + 1, :]


def exchange_kernel(
    group, half, rows, idx_ref, temp_ref, mix_ref, query_ref, over_ref, col_ref, off_ref, key_hbm, head_hbm,
    out_ref, sum_ref,
    key_buf, head_buf, turned, score, send, relay, recv, rcol, roff, off_smem, knn_stat, lm_stat, rknn, rlm,
    logit, hist, piece_a, piece_b,
    key_sem, head_sem, data_send, data_recv, relay_send, relay_recv, col_send, col_recv, off_send, off_recv,
    knn_send, knn_recv, lm_send, lm_recv, own_sem,
):
    me = lax.axis_index("model")
    n_local, vocab = key_hbm.shape[0], head_hbm.shape[0]
    slots = rows * LANES
    mid, quarter = group // 2, group // 4

    def peer(k):
        return {"model": lax.rem(me + k, group)}

    barrier = pltpu.get_barrier_semaphore()
    for k in range(1, group):
        pl.semaphore_signal(barrier, inc=1, device_id=peer(k), device_id_type=MESH)

    def key_copy(step):
        return pltpu.make_async_copy(
            key_hbm.at[pl.ds(step * KEY_TILE, KEY_TILE), :],
            key_buf.at[lax.rem(step, KEY_BUFS)],
            key_sem.at[lax.rem(step, KEY_BUFS)],
        )

    head_full = vocab // HEAD_TILE
    head_rest = vocab - head_full * HEAD_TILE

    def head_copy(step):
        return pltpu.make_async_copy(
            head_hbm.at[pl.ds(step * HEAD_TILE, HEAD_TILE), :],
            head_buf.at[lax.rem(step, HEAD_BUFS)],
            head_sem.at[lax.rem(step, HEAD_BUFS)],
        )

    key_steps = n_local // KEY_TILE
    for step in range(KEY_BUFS - 1):
        key_copy(step).start()

    temp = temp_ref[0]
    query = query_ref[...].astype(jnp.float32)
    turned[...] = jnp.concatenate([query, query], axis=0).T.astype(jnp.bfloat16)

    def merge(total, tile):
        top, acc = total
        new = jnp.maximum(top, jnp.max(tile, axis=0, keepdims=True))
        acc = acc * jnp.exp(top - new) + jnp.sum(jnp.exp(tile - new), axis=0, keepdims=True)
        return new, acc

    empty = (jnp.full((1, LANES), -3e38, jnp.float32), jnp.zeros((1, LANES), jnp.float32))

    def score_step(step, total):
        @pl.when(step + KEY_BUFS - 1 < key_steps)
        def _():
            key_copy(step + KEY_BUFS - 1).start()

        key_copy(step).wait()
        keys = key_buf[lax.rem(step, KEY_BUFS)]
        cross = jnp.dot(keys, turned[...], preferred_element_type=jnp.float32)
        wide = keys.astype(jnp.float32)
        square = jnp.sum(wide * wide, axis=1, keepdims=True)
        tile = (2.0 * cross - square) / temp
        score[pl.ds(pl.multiple_of(step * KEY_TILE, KEY_TILE), KEY_TILE), :] = tile
        return merge(total, tile)

    knn_max, knn_sum = lax.fori_loop(0, key_steps, score_step, empty)
    knn_stat[0:1, :] = knn_max
    knn_stat[1:2, :] = knn_sum
    knn_stat[2:8, :] = over_ref[2:8, :]

    for step in range(HEAD_BUFS - 1):
        head_copy(step).start()

    pl.semaphore_wait(barrier, group - 1)

    left = lax.broadcasted_iota(jnp.int32, (1, LANES), 1) < LANES // 2

    def remote(src, dst, send_sem, recv_sem, k):
        return pltpu.make_async_remote_copy(
            src_ref=src, dst_ref=dst, send_sem=send_sem, recv_sem=recv_sem,
            device_id=peer(k), device_id_type=MESH,
        )

    def data_copy(k):
        return remote(send.at[k], recv[k], data_send.at[k], data_recv.at[k], k)

    def cols_copy(k):
        return remote(col_ref.at[lax.rem(me + k, group)], rcol.at[k], col_send.at[k], col_recv.at[k], k)

    def offs_copy(k):
        return remote(off_ref.at[lax.rem(me + k, group)], roff.at[k], off_send.at[k], off_recv.at[k], k)

    def knn_copy(k):
        return remote(knn_stat, rknn.at[k], knn_send.at[k], knn_recv.at[k], k)

    def lm_copy(k):
        return remote(lm_stat, rlm.at[k], lm_send.at[k], lm_recv.at[k], k)

    first_leg = remote(send.at[mid], relay, relay_send, relay_recv, group - quarter)
    second_leg = remote(relay, recv[mid], data_send.at[mid], data_recv.at[mid], group - quarter)

    def pack(k, target, at):
        base = lax.rem(me + k, group) * slots

        def tile(t, carry):
            for i in range(8):
                j = t * 8 + i
                a = idx_ref[base + j]
                b = idx_ref[base + half + j]
                row = jnp.where(left, score[pl.ds(a, 1), :], score[pl.ds(b, 1), :])
                if at is None:
                    target[pl.ds(j, 1), :] = row
                else:
                    target[at, pl.ds(j, 1), :] = row
            return carry

        lax.fori_loop(0, half // 8, tile, 0)

    for k in range(1, group):
        cols_copy(k).start()
        offs_copy(k).start()
    order = [mid]
    for k in range(1, mid):
        order += [mid - k, mid + k]
    waiting = None
    for k in order:
        pack(k, send, k)
        if waiting is not None:
            waiting.start()
        waiting = first_leg if k == mid else data_copy(k)
    pack(0, recv[0], None)
    waiting.start()
    for k in range(1, group):
        knn_copy(k).start()
    own = [
        pltpu.make_async_copy(col_ref.at[me], rcol.at[0], own_sem.at[0]),
        pltpu.make_async_copy(off_ref.at[me], roff.at[0], own_sem.at[1]),
        pltpu.make_async_copy(knn_stat, rknn.at[0], own_sem.at[2]),
    ]
    for copy in own:
        copy.start()
    first_leg.wait()
    second_leg.start()

    def head_tile(tile, where):
        tile = jnp.dot(tile, turned[...], preferred_element_type=jnp.float32)
        logit[where, :] = tile
        return tile

    rest_copy = pltpu.make_async_copy(
        head_hbm.at[pl.ds(head_full * HEAD_TILE, head_rest), :],
        head_buf.at[HEAD_BUFS, pl.ds(0, head_rest), :],
        head_sem.at[HEAD_BUFS],
    )
    if head_rest:
        rest_copy.start()

    def head_step(step, total):
        @pl.when(step + HEAD_BUFS - 1 < head_full)
        def _():
            head_copy(step + HEAD_BUFS - 1).start()

        head_copy(step).wait()
        where = pl.ds(pl.multiple_of(step * HEAD_TILE, HEAD_TILE), HEAD_TILE)
        return merge(total, head_tile(head_buf[lax.rem(step, HEAD_BUFS)], where))

    total = lax.fori_loop(0, head_full, head_step, empty)
    if head_rest:
        rest_copy.wait()
        where = pl.ds(head_full * HEAD_TILE, head_rest)
        total = merge(total, head_tile(head_buf[HEAD_BUFS, :head_rest, :], where))
    lm_stat[0:1, :] = total[0]
    lm_stat[1:2, :] = total[1]
    lm_stat[2:8, :] = jnp.zeros((6, LANES), jnp.float32)
    hist[...] = jnp.zeros_like(hist)
    for pieces in (piece_a, piece_b):
        pieces[:, 2 * half :, :] = jnp.zeros((BATCH, WINDOW, LANES), jnp.float32)
    own.append(pltpu.make_async_copy(lm_stat, rlm.at[0], own_sem.at[3]))
    own[-1].start()
    for k in range(1, group):
        lm_copy(k).start()

    def combine(stat):
        top = stat[0, 0:1, :]
        for k in range(1, group):
            top = jnp.maximum(top, stat[k, 0:1, :])
        acc = jnp.zeros((1, LANES), jnp.float32)
        for k in range(group):
            acc = acc + stat[k, 1:2, :] * jnp.exp(stat[k, 0:1, :] - top)
        return top, acc

    for copy in own:
        copy.wait()
    for k in range(1, group):
        cols_copy(k).wait()
        offs_copy(k).wait()
        knn_copy(k).wait()
    to_smem = pltpu.make_async_copy(roff, off_smem, own_sem.at[0])
    to_smem.start()
    knn_max, knn_sum = combine(rknn)
    over = rknn[0, 2:3, :]
    for k in range(1, group):
        over = jnp.maximum(over, rknn[k, 2:3, :])
    to_smem.wait()

    lane = lax.broadcasted_iota(jnp.int32, (1, LANES), 1)
    column = lax.broadcasted_iota(jnp.int32, (COLS, LANES), 0)

    def split(where_i, start, value):
        high = value.astype(jnp.bfloat16).astype(jnp.float32)
        rest = value - high
        middle = rest.astype(jnp.bfloat16).astype(jnp.float32)
        piece_a[where_i, pl.ds(start, 8), :] = jnp.where(left, high, middle)
        piece_b[where_i, pl.ds(start, 8), :] = rest - middle

    def add_batch(members):
        for i, k in enumerate(members):

            def unpack(t, carry):
                start = pl.multiple_of(t * 8, 8)
                value = jnp.exp(recv[k][pl.ds(start, 8), :] - knn_max)
                other = pltpu.roll(value, LANES // 2, 1)
                split(i, start, jnp.where(left, value, other))
                split(i, pl.multiple_of(half + start, 8), jnp.where(left, other, value))
                return carry

            lax.fori_loop(0, half // 8, unpack, 0)

        def one_group(g, carry):
            values, hots = [], []
            pair = []
            for i, k in enumerate(members):
                start = off_smem[k, 0, g]
                values.append(
                    jnp.concatenate(
                        [
                            piece_a[i, pl.ds(start, WINDOW), :].astype(jnp.bfloat16),
                            piece_b[i, pl.ds(start, WINDOW), :].astype(jnp.bfloat16),
                        ],
                        axis=1,
                    )
                )
                row, off = start // LANES, start % LANES
                low = rcol[k, pl.ds(row, 1), :]
                high = rcol[k, pl.ds(jnp.minimum(row + 1, rows - 1), 1), :]
                shift = (2 * LANES - off + WINDOW * (i % 2)) % LANES
                seen = jnp.where(lane < off, high, low)
                pair.append(pltpu.roll(seen, shift, 1))
                if i % 2:
                    cols = jnp.where(left, pair[i - 1], pair[i]) - g * COLS
                    hots.append(jnp.where(column == cols, 1.0, 0.0).astype(jnp.bfloat16))
            part = jnp.dot(
                jnp.concatenate(hots, axis=1), jnp.concatenate(values, axis=0),
                preferred_element_type=jnp.float32,
            )
            where = pl.ds(pl.multiple_of(g * COLS, COLS), COLS)
            both = part[:, :LANES]
            hist[where, :] += both + pltpu.roll(both, LANES // 2, 1) + part[:, LANES:]
            return carry

        lax.fori_loop(0, hist.shape[0] // COLS, one_group, 0, unroll=2)

    queue = [0] + [k for k in order if k != mid]
    queue.insert(max(len(queue) - BATCH, 1), mid)
    for at in range(0, group, BATCH):
        members = queue[at : at + BATCH]
        for k in members:
            if k == mid:
                second_leg.wait()
            elif k:
                data_copy(k).wait()
        add_batch(members)

    for k in range(1, group):
        lm_copy(k).wait()
    lm_max, lm_sum = combine(rlm)
    sum_ref[0:1, :] = knn_max
    sum_ref[1:2, :] = knn_sum
    sum_ref[2:3, :] = lm_max
    sum_ref[3:4, :] = lm_sum
    sum_ref[4:8, :] = jnp.broadcast_to(over, (4, LANES))

    mix = mix_ref[0]
    knn_scale = mix / knn_sum
    lm_scale = (1.0 - mix) / lm_sum

    def tile(start, count):
        where = pl.ds(start, count)
        prob = hist[where, :] * knn_scale + jnp.exp(logit[where, :] - lm_max) * lm_scale
        return jnp.log(prob)

    full = vocab // LANES

    def write(i, carry):
        start = pl.multiple_of(i * LANES, LANES)
        out_ref[:, pl.ds(start, LANES)] = tile(start, LANES).T[: LANES // 2, :]
        return carry

    lax.fori_loop(0, full, write, 0)
    rest = vocab - full * LANES
    if rest:
        last = jnp.concatenate(
            [tile(full * LANES, rest), jnp.zeros((LANES - rest, LANES), jnp.float32)], axis=0
        )
        out_ref[:, full * LANES :] = last.T[: LANES // 2, :rest]


def solution(mesh):
    group = mesh.shape["model"]

    def local_step(queries, w_shard, key_shard, tok_shard, temperature, mix_weight):
        row_count, depth = queries.shape
        vocab, n_local = w_shard.shape[1], key_shard.shape[0]
        mean = n_local / group
        cap = round_up(int(mean + 4.5 * math.sqrt(mean)), 16)
        half = cap // 2
        slot_rows = round_up(cap, LANES) // LANES
        slots = slot_rows * LANES
        groups = round_up(vocab, 2 * COLS) // COLS

        order_tok, order_idx = lax.sort(
            (tok_shard, lax.iota(jnp.int32, n_local)), num_keys=1, is_stable=False
        )
        pad = (slot_rows + 8) * LANES
        fill = jnp.zeros((pad,), jnp.int32)
        shape_2d = ((n_local + pad) // LANES, LANES)
        tok_2d = jnp.concatenate([order_tok, fill]).reshape(shape_2d)
        idx_2d = jnp.concatenate([order_idx, fill]).reshape(shape_2d)

        smem = pl.BlockSpec(memory_space=pltpu.SMEM)
        vmem = pl.BlockSpec(memory_space=pltpu.VMEM)
        hbm = pl.BlockSpec(memory_space=pl.ANY)
        cols, idx, offs, over = pl.pallas_call(
            functools.partial(slot_kernel, group, vocab, cap, slot_rows, n_local),
            out_shape=(
                jax.ShapeDtypeStruct((group, slot_rows, LANES), jnp.int32),
                jax.ShapeDtypeStruct((group * slot_rows, LANES), jnp.int32),
                jax.ShapeDtypeStruct((group, 1, LANES), jnp.int32),
                jax.ShapeDtypeStruct((8, LANES), jnp.float32),
            ),
            in_specs=[vmem, vmem],
            out_specs=(vmem, vmem, vmem, vmem),
            name="slots",
        )(tok_2d, idx_2d)

        stat = pltpu.VMEM((8, LANES), jnp.float32)
        stats = pltpu.VMEM((group, 8, LANES), jnp.float32)
        pieces = pltpu.VMEM((BATCH, 2 * half + WINDOW, LANES), jnp.float32)
        dma = pltpu.SemaphoreType.DMA
        chunk = pltpu.VMEM((half, LANES), jnp.float32)
        fast, sums = pl.pallas_call(
            functools.partial(exchange_kernel, group, half, slot_rows),
            out_shape=(
                jax.ShapeDtypeStruct((row_count, vocab), jnp.float32),
                jax.ShapeDtypeStruct((8, LANES), jnp.float32),
            ),
            in_specs=[smem, smem, smem, vmem, vmem, vmem, vmem, hbm, hbm],
            out_specs=(vmem, vmem),
            scratch_shapes=[
                pltpu.VMEM((KEY_BUFS, KEY_TILE, depth), jnp.bfloat16),
                pltpu.VMEM((HEAD_BUFS + 1, HEAD_TILE, depth), jnp.bfloat16),
                pltpu.VMEM((depth, LANES), jnp.bfloat16),
                pltpu.VMEM((n_local, LANES), jnp.float32),
                pltpu.VMEM((group, half, LANES), jnp.float32),
                chunk,
                [chunk] * group,
                pltpu.VMEM((group, slot_rows, LANES), jnp.int32),
                pltpu.VMEM((group, 1, LANES), jnp.int32),
                pltpu.SMEM((group, 1, LANES), jnp.int32),
                stat, stat, stats, stats,
                pltpu.VMEM((vocab, LANES), jnp.float32),
                pltpu.VMEM((groups * COLS, LANES), jnp.float32),
                pieces, pieces,
                dma((KEY_BUFS,)), dma((HEAD_BUFS + 1,)), dma((group,)), dma((group,)), dma, dma,
                dma((group,)), dma((group,)), dma((group,)), dma((group,)),
                dma((group,)), dma((group,)), dma((group,)), dma((group,)), dma((4,)),
            ],
            compiler_params=pltpu.CompilerParams(
                collective_id=0, has_side_effects=True, vmem_limit_bytes=VMEM_LIMIT
            ),
            name="exchange",
        )(idx.reshape(-1), temperature, mix_weight, queries, over, cols, offs, key_shard, w_shard.T)

        def dense(unused):
            me = lax.axis_index("model")
            row_max, row_total = sums[0, :row_count], sums[1, :row_count]
            lm_max, lm_total = sums[2, :row_count], sums[3, :row_count]
            cross_dot = jnp.einsum("bd,nd->nb", queries, key_shard, preferred_element_type=jnp.float32)
            key_sq = jnp.sum(jnp.square(key_shard.astype(jnp.float32)), axis=1)
            scores = (2.0 * cross_dot - key_sq[:, None]) / temperature[0]
            weights = jnp.exp(scores - row_max[None, :])
            ring = [(i, (i + 1) % group) for i in range(group)]

            def turn(k, acc):
                acc = lax.ppermute(acc, "model", ring)
                col = tok_shard - lax.rem(me + group - 1 - k, group) * vocab
                col = jnp.where((col >= 0) & (col < vocab), col, vocab)
                return acc.at[col].add(weights)

            acc = jnp.zeros((vocab + 1, row_count), jnp.float32)
            acc = lax.fori_loop(0, group, turn, acc)
            logit = jnp.dot(queries, w_shard, preferred_element_type=jnp.float32)
            p_lm = jnp.exp(logit - lm_max[:, None]) / lm_total[:, None]
            p_knn = acc[:vocab].T / row_total[:, None]
            mix_value = mix_weight[0]
            return jnp.log(mix_value * p_knn + (1.0 - mix_value) * p_lm)

        return lax.cond(sums[4, 0] > 0.0, dense, lambda kept: kept, fast)

    return jax.shard_map(
        local_step,
        mesh=mesh,
        in_specs=(P("data", None), P(None, "model"), P("model", None), P("model"), P(), P()),
        out_specs=P("data", "model"),
        check_vma=False,
    )
```

time: 251 us -> 309 us (1.23)
  the two profiles are of different devices: /device:TPU:21 before, /device:TPU:55 now
where the time goes in v2:
time: 309 us; the launch traced here: 308 us
  Pallas kernels  294 us (95%)
  other arithmetic  7.28 us (2%)
  local copies, waits for them, and re-layouts  4.48 us (1%)
    pallas_call x1, Pallas kernels, local_step(): pl.pallas_call(functools.partial(exchange_kernel, group, half, slot_rows)...  291 us
    sort x1, other arithmetic, local_step(): lax.sort((tok_shard, lax.iota(jnp.int32, n_local)), num_keys=1, is_stable...  7.28 us

profile of v2, /device:TPU:55, one launch (start us, length us, event | category | flops | bytes accessed | tf_op | source)
XLA Modules:
  0.0 308.3 jit_solution(13261941928459046536)
XLA Ops:
  0.0 7.3 %sort.15 = (s32[16384]{0:T(1024)S(1)}, s32[16384]{0:T(1024)S(1)}) sort(s32[16384]{0:T(1024)} %param.13, s32[16384]{0:T(1024)S(1)} %iota.3), dimensions={0}, to_apply=%region_0.0 | sort | flops 229376 | bytes 262144 | tf_op jit(solution)/shard_map/sort | solution.py:390
  7.3 0.7 pad_bitcast_fusion
  8.0 3.9 %slots.1 = (s32[16,10,128]{2,1,0:T(8,128)}, s32[160,128]{1,0:T(8,128)}, s32[16,1,128]{2,1,0:T(1,128)}, f32[8,128]{1,0:T(8,128)}) custom-call(s32[146,128]{1,0:T(8,128)} %get-tuple-element.235.tok_ref, s32[146,128]{1,0:T(8,128)} %get-tuple-element.234.ord_ref), custom_call_target="tpu_custom_call" | custom-call | tf_op jit(solution)/shard_map/slots/pallas_call | solution.py:402
  13.2 0.0 copy-start.1
  13.2 290.5 %exchange.1 = (f32[64,9496]{1,0:T(8,128)}, f32[8,128]{1,0:T(8,128)S(1)}) custom-call(s32[20480]{0:T(1024)} %bitcast.34, f32[1]{0:T(128)S(6)} %copy.36.temp_ref, f32[1]{0:T(128)S(6)} %copy.37.mix_ref, bf16[64,1536]{1,0:T(8,128)(2,1)} %query_ref.1, f32[8,128]{1,0:T(8,128)} %get-tuple-element.171.over_ref, s32[16,10,128]{2,1,0:T(8,128)} %get-tuple-element.172.col_ref, ...), custom_call_target="tpu_custom_call" | custom-call | tf_op jit(solution)/shard_map/exchange/pallas_call | solution.py:420
  303.7 0.5 slice.18
  304.8 0.0 copy-done.1
  304.9 0.2 conditional.1
  305.1 3.3 %copy.38 = f32[64,9496]{1,0:T(8,128)} copy(f32[64,9496]{1,0:T(8,128)} %get-tuple-element.176) | data formatting | bytes 4861952
  (1 shorter events, 0.0 us)
Async XLA Ops:
  13.2 291.7 %copy-start.1 = (bf16[64,1536]{1,0:T(8,128)(2,1)S(1)}, bf16[64,1536]{1,0:T(8,128)(2,1)}, u32[]{:S(2)}) copy-start(bf16[64,1536]{1,0:T(8,128)(2,1)} %query_ref.1) | copy-start | bytes 589828

commit v3 on v2

--- a/solution.py
+++ b/solution.py
@@ -24,7 +24,7 @@
     return (value + step - 1) // step * step
 
 
-def slot_kernel(group, vocab, cap, rows, n_local, tok_ref, ord_ref, col_ref, idx_ref, off_ref, over_ref):
+def slot_kernel(group, vocab, cap, rows, n_local, tok_ref, ord_ref, col_ref, idx_ref, over_ref):
     lane = lax.broadcasted_iota(jnp.int32, (rows, LANES), 1)
     slot = lax.broadcasted_iota(jnp.int32, (rows, LANES), 0) * LANES + lane
     bound = lax.broadcasted_iota(jnp.int32, (LANES, LANES), 0)
@@ -50,7 +50,7 @@
 
         used = slot < count
         col = jnp.where(used, shifted(tok_ref) - d * vocab, vocab)
-        col_ref[d] = col
+        col_ref[d, :rows, :] = col
         idx_ref[d * rows : (d + 1) * rows, :] = jnp.where(used, shifted(ord_ref), 0)
         first = jnp.where(used, col // COLS, LANES)
         hits = jnp.zeros((LANES, LANES), jnp.float32)
@@ -62,16 +62,15 @@
     over_ref[...] = jnp.full((8, LANES), over, jnp.float32)
     turned = jnp.minimum(table, float(cap)).T.astype(jnp.int32)
     for d in range(group):
-        off_ref[d] = turned[d : d + 1, :]
+        col_ref[d, rows : rows + 1, :] = turned[d : d + 1, :]
 
 
 def exchange_kernel(
-    group, half, rows, idx_ref, temp_ref, mix_ref, query_ref, over_ref, col_ref, off_ref, key_hbm, head_hbm,
-    out_ref, sum_ref,
-    key_buf, head_buf, turned, score, send, relay, recv, rcol, roff, off_smem, knn_stat, lm_stat, rknn, rlm,
-    logit, hist, piece_a, piece_b,
-    key_sem, head_sem, data_send, data_recv, relay_send, relay_recv, col_send, col_recv, off_send, off_recv,
-    knn_send, knn_recv, lm_send, lm_recv, own_sem,
+    group, half, rows, idx_ref, temp_ref, query_ref, over_ref, col_ref, key_hbm, head_hbm,
+    recv_hbm, rcol_hbm, rstat_hbm, logit_hbm,
+    key_buf, head_buf, turned, score, send, relay, stat, logit,
+    key_sem, head_sem, data_send, data_recv, relay_send, relay_recv, col_send, col_recv,
+    stat_send, stat_recv, own_sem,
 ):
     me = lax.axis_index("model")
     n_local, vocab = key_hbm.shape[0], head_hbm.shape[0]
@@ -133,9 +132,6 @@
         return merge(total, tile)
 
     knn_max, knn_sum = lax.fori_loop(0, key_steps, score_step, empty)
-    knn_stat[0:1, :] = knn_max
-    knn_stat[1:2, :] = knn_sum
-    knn_stat[2:8, :] = over_ref[2:8, :]
 
     for step in range(HEAD_BUFS - 1):
         head_copy(step).start()
@@ -151,24 +147,18 @@
         )
 
     def data_copy(k):
-        return remote(send.at[k], recv[k], data_send.at[k], data_recv.at[k], k)
+        return remote(send.at[k], recv_hbm.at[k], data_send.at[k], data_recv.at[k], k)
 
     def cols_copy(k):
-        return remote(col_ref.at[lax.rem(me + k, group)], rcol.at[k], col_send.at[k], col_recv.at[k], k)
-
-    def offs_copy(k):
-        return remote(off_ref.at[lax.rem(me + k, group)], roff.at[k], off_send.at[k], off_recv.at[k], k)
-
-    def knn_copy(k):
-        return remote(knn_stat, rknn.at[k], knn_send.at[k], knn_recv.at[k], k)
-
-    def lm_copy(k):
-        return remote(lm_stat, rlm.at[k], lm_send.at[k], lm_recv.at[k], k)
+        return remote(col_ref.at[lax.rem(me + k, group)], rcol_hbm.at[k], col_send.at[k], col_recv.at[k], k)
+
+    def stat_copy(k):
+        return remote(stat, rstat_hbm.at[k], stat_send.at[k], stat_recv.at[k], k)
 
     first_leg = remote(send.at[mid], relay, relay_send, relay_recv, group - quarter)
-    second_leg = remote(relay, recv[mid], data_send.at[mid], data_recv.at[mid], group - quarter)
-
-    def pack(k, target, at):
+    second_leg = remote(relay, recv_hbm.at[mid], data_send.at[mid], data_recv.at[mid], group - quarter)
+
+    def pack(k):
         base = lax.rem(me + k, group) * slots
 
         def tile(t, carry):
@@ -177,37 +167,24 @@
                 a = idx_ref[base + j]
                 b = idx_ref[base + half + j]
                 row = jnp.where(left, score[pl.ds(a, 1), :], score[pl.ds(b, 1), :])
-                if at is None:
-                    target[pl.ds(j, 1), :] = row
-                else:
-                    target[at, pl.ds(j, 1), :] = row
+                send[k, pl.ds(j, 1), :] = row
             return carry
 
         lax.fori_loop(0, half // 8, tile, 0)
 
     for k in range(1, group):
         cols_copy(k).start()
-        offs_copy(k).start()
     order = [mid]
     for k in range(1, mid):
         order += [mid - k, mid + k]
     waiting = None
     for k in order:
-        pack(k, send, k)
+        pack(k)
         if waiting is not None:
             waiting.start()
         waiting = first_leg if k == mid else data_copy(k)
-    pack(0, recv[0], None)
+    pack(0)
     waiting.start()
-    for k in range(1, group):
-        knn_copy(k).start()
-    own = [
-        pltpu.make_async_copy(col_ref.at[me], rcol.at[0], own_sem.at[0]),
-        pltpu.make_async_copy(off_ref.at[me], roff.at[0], own_sem.at[1]),
-        pltpu.make_async_copy(knn_stat, rknn.at[0], own_sem.at[2]),
-    ]
-    for copy in own:
-        copy.start()
     first_leg.wait()
     second_leg.start()
 
@@ -238,68 +215,104 @@
         rest_copy.wait()
         where = pl.ds(head_full * HEAD_TILE, head_rest)
         total = merge(total, head_tile(head_buf[HEAD_BUFS, :head_rest, :], where))
-    lm_stat[0:1, :] = total[0]
-    lm_stat[1:2, :] = total[1]
-    lm_stat[2:8, :] = jnp.zeros((6, LANES), jnp.float32)
+
+    stat[0:1, :] = knn_max
+    stat[1:2, :] = knn_sum
+    stat[2:3, :] = total[0]
+    stat[3:4, :] = total[1]
+    stat[4:8, :] = over_ref[4:8, :]
+    own = [
+        pltpu.make_async_copy(send.at[0], recv_hbm.at[0], own_sem.at[0]),
+        pltpu.make_async_copy(col_ref.at[me], rcol_hbm.at[0], own_sem.at[1]),
+        pltpu.make_async_copy(logit, logit_hbm, own_sem.at[2]),
+        pltpu.make_async_copy(stat, rstat_hbm.at[0], own_sem.at[3]),
+    ]
+    for copy in own:
+        copy.start()
+    for k in range(1, group):
+        stat_copy(k).start()
+    for copy in own:
+        copy.wait()
+    for k in range(1, group):
+        stat_copy(k).wait()
+        cols_copy(k).wait()
+        if k == mid:
+            second_leg.wait()
+        else:
+            data_copy(k).wait()
+
+
+def finish_kernel(
+    group, half, rows, off_smem, mix_ref, rcol, stat, recv_hbm, logit_hbm, out_ref, sum_ref,
+    recv, logit, hist, piece_a, piece_b, recv_sem, logit_sem,
+):
+    vocab = logit_hbm.shape[0]
+    batches = group // BATCH
+
+    def fetch(b):
+        where = pl.ds(b * BATCH, BATCH)
+        return pltpu.make_async_copy(recv_hbm.at[where], recv.at[where], recv_sem.at[b])
+
+    for b in range(batches):
+        fetch(b).start()
+    fetch_logit = pltpu.make_async_copy(logit_hbm, logit, logit_sem)
+    fetch_logit.start()
+
+    def combine(row):
+        top = stat[0, row : row + 1, :]
+        for k in range(1, group):
+            top = jnp.maximum(top, stat[k, row : row + 1, :])
+        acc = jnp.zeros((1, LANES), jnp.float32)
+        for k in range(group):
+            acc = acc + stat[k, row + 1 : row + 2, :] * jnp.exp(stat[k, row : row + 1, :] - top)
+        return top, acc
+
+    knn_max, knn_sum = combine(0)
+    lm_max, lm_sum = combine(2)
+    over = stat[0, 4:5, :]
+    for k in range(1, group):
+        over = jnp.maximum(over, stat[k, 4:5, :])
+    sum_ref[0:1, :] = knn_max
+    sum_ref[1:2, :] = knn_sum
+    sum_ref[2:3, :] = lm_max
+    sum_ref[3:4, :] = lm_sum
+    sum_ref[4:8, :] = jnp.broadcast_to(over, (4, LANES))
+
     hist[...] = jnp.zeros_like(hist)
     for pieces in (piece_a, piece_b):
         pieces[:, 2 * half :, :] = jnp.zeros((BATCH, WINDOW, LANES), jnp.float32)
-    own.append(pltpu.make_async_copy(lm_stat, rlm.at[0], own_sem.at[3]))
-    own[-1].start()
-    for k in range(1, group):
-        lm_copy(k).start()
-
-    def combine(stat):
-        top = stat[0, 0:1, :]
-        for k in range(1, group):
-            top = jnp.maximum(top, stat[k, 0:1, :])
-        acc = jnp.zeros((1, LANES), jnp.float32)
-        for k in range(group):
-            acc = acc + stat[k, 1:2, :] * jnp.exp(stat[k, 0:1, :] - top)
-        return top, acc
-
-    for copy in own:
-        copy.wait()
-    for k in range(1, group):
-        cols_copy(k).wait()
-        offs_copy(k).wait()
-        knn_copy(k).wait()
-    to_smem = pltpu.make_async_copy(roff, off_smem, own_sem.at[0])
-    to_smem.start()
-    knn_max, knn_sum = combine(rknn)
-    over = rknn[0, 2:3, :]
-    for k in range(1, group):
-        over = jnp.maximum(over, rknn[k, 2:3, :])
-    to_smem.wait()
 
     lane = lax.broadcasted_iota(jnp.int32, (1, LANES), 1)
+    left = lane < LANES // 2
     column = lax.broadcasted_iota(jnp.int32, (COLS, LANES), 0)
 
-    def split(where_i, start, value):
+    def split(i, start, count, value):
         high = value.astype(jnp.bfloat16).astype(jnp.float32)
         rest = value - high
         middle = rest.astype(jnp.bfloat16).astype(jnp.float32)
-        piece_a[where_i, pl.ds(start, 8), :] = jnp.where(left, high, middle)
-        piece_b[where_i, pl.ds(start, 8), :] = rest - middle
-
-    def add_batch(members):
-        for i, k in enumerate(members):
+        piece_a[i, pl.ds(start, count), :] = jnp.where(left, high, middle)
+        piece_b[i, pl.ds(start, count), :] = rest - middle
+
+    def one_batch(b, carry):
+        fetch(b).wait()
+        for i in range(BATCH):
 
             def unpack(t, carry):
                 start = pl.multiple_of(t * 8, 8)
-                value = jnp.exp(recv[k][pl.ds(start, 8), :] - knn_max)
+                value = jnp.exp(recv[b * BATCH + i, pl.ds(start, 8), :] - knn_max)
                 other = pltpu.roll(value, LANES // 2, 1)
-                split(i, start, jnp.where(left, value, other))
-                split(i, pl.multiple_of(half + start, 8), jnp.where(left, other, value))
+                split(i, start, 8, jnp.where(left, value, other))
+                split(i, pl.multiple_of(half + start, 8), 8, jnp.where(left, other, value))
                 return carry
 
-            lax.fori_loop(0, half // 8, unpack, 0)
+            lax.fori_loop(0, half // 8, unpack, 0, unroll=4)
 
         def one_group(g, carry):
             values, hots = [], []
             pair = []
-            for i, k in enumerate(members):
-                start = off_smem[k, 0, g]
+            for i in range(BATCH):
+                k = b * BATCH + i
+                start = off_smem[k * LANES + g]
                 values.append(
                     jnp.concatenate(
                         [
@@ -328,26 +341,10 @@
             return carry
 
         lax.fori_loop(0, hist.shape[0] // COLS, one_group, 0, unroll=2)
-
-    queue = [0] + [k for k in order if k != mid]
-    queue.insert(max(len(queue) - BATCH, 1), mid)
-    for at in range(0, group, BATCH):
-        members = queue[at : at + BATCH]
-        for k in members:
-            if k == mid:
-                second_leg.wait()
-            elif k:
-                data_copy(k).wait()
-        add_batch(members)
-
-    for k in range(1, group):
-        lm_copy(k).wait()
-    lm_max, lm_sum = combine(rlm)
-    sum_ref[0:1, :] = knn_max
-    sum_ref[1:2, :] = knn_sum
-    sum_ref[2:3, :] = lm_max
-    sum_ref[3:4, :] = lm_sum
-    sum_ref[4:8, :] = jnp.broadcast_to(over, (4, LANES))
+        return carry
+
+    lax.fori_loop(0, batches, one_batch, 0)
+    fetch_logit.wait()
 
     mix = mix_ref[0]
     knn_scale = mix / knn_sum
@@ -399,32 +396,32 @@
         smem = pl.BlockSpec(memory_space=pltpu.SMEM)
         vmem = pl.BlockSpec(memory_space=pltpu.VMEM)
         hbm = pl.BlockSpec(memory_space=pl.ANY)
-        cols, idx, offs, over = pl.pallas_call(
+        table = jax.ShapeDtypeStruct((group, slot_rows + 1, LANES), jnp.int32)
+        cols, idx, over = pl.pallas_call(
             functools.partial(slot_kernel, group, vocab, cap, slot_rows, n_local),
             out_shape=(
-                jax.ShapeDtypeStruct((group, slot_rows, LANES), jnp.int32),
+                table,
                 jax.ShapeDtypeStruct((group * slot_rows, LANES), jnp.int32),
-                jax.ShapeDtypeStruct((group, 1, LANES), jnp.int32),
                 jax.ShapeDtypeStruct((8, LANES), jnp.float32),
             ),
             in_specs=[vmem, vmem],
-            out_specs=(vmem, vmem, vmem, vmem),
+            out_specs=(vmem, vmem, vmem),
             name="slots",
         )(tok_2d, idx_2d)
 
-        stat = pltpu.VMEM((8, LANES), jnp.float32)
-        stats = pltpu.VMEM((group, 8, LANES), jnp.float32)
-        pieces = pltpu.VMEM((BATCH, 2 * half + WINDOW, LANES), jnp.float32)
         dma = pltpu.SemaphoreType.DMA
         chunk = pltpu.VMEM((half, LANES), jnp.float32)
-        fast, sums = pl.pallas_call(
+        logit = pltpu.VMEM((vocab, LANES), jnp.float32)
+        recv, rcols, rstat, logits = pl.pallas_call(
             functools.partial(exchange_kernel, group, half, slot_rows),
             out_shape=(
-                jax.ShapeDtypeStruct((row_count, vocab), jnp.float32),
-                jax.ShapeDtypeStruct((8, LANES), jnp.float32),
+                jax.ShapeDtypeStruct((group, half, LANES), jnp.float32),
+                table,
+                jax.ShapeDtypeStruct((group, 8, LANES), jnp.float32),
+                jax.ShapeDtypeStruct((vocab, LANES), jnp.float32),
             ),
-            in_specs=[smem, smem, smem, vmem, vmem, vmem, vmem, hbm, hbm],
-            out_specs=(vmem, vmem),
+            in_specs=[smem, smem, vmem, vmem, vmem, hbm, hbm],
+            out_specs=(hbm, hbm, hbm, hbm),
             scratch_shapes=[
                 pltpu.VMEM((KEY_BUFS, KEY_TILE, depth), jnp.bfloat16),
                 pltpu.VMEM((HEAD_BUFS + 1, HEAD_TILE, depth), jnp.bfloat16),
@@ -432,23 +429,35 @@
                 pltpu.VMEM((n_local, LANES), jnp.float32),
                 pltpu.VMEM((group, half, LANES), jnp.float32),
                 chunk,
-                [chunk] * group,
-                pltpu.VMEM((group, slot_rows, LANES), jnp.int32),
-                pltpu.VMEM((group, 1, LANES), jnp.int32),
-                pltpu.SMEM((group, 1, LANES), jnp.int32),
-                stat, stat, stats, stats,
-                pltpu.VMEM((vocab, LANES), jnp.float32),
-                pltpu.VMEM((groups * COLS, LANES), jnp.float32),
-                pieces, pieces,
+                pltpu.VMEM((8, LANES), jnp.float32),
+                logit,
                 dma((KEY_BUFS,)), dma((HEAD_BUFS + 1,)), dma((group,)), dma((group,)), dma, dma,
-                dma((group,)), dma((group,)), dma((group,)), dma((group,)),
                 dma((group,)), dma((group,)), dma((group,)), dma((group,)), dma((4,)),
             ],
             compiler_params=pltpu.CompilerParams(
                 collective_id=0, has_side_effects=True, vmem_limit_bytes=VMEM_LIMIT
             ),
             name="exchange",
-        )(idx.reshape(-1), temperature, mix_weight, queries, over, cols, offs, key_shard, w_shard.T)
+        )(idx.reshape(-1), temperature, queries, over, cols, key_shard, w_shard.T)
+
+        pieces = pltpu.VMEM((BATCH, 2 * half + WINDOW, LANES), jnp.float32)
+        fast, sums = pl.pallas_call(
+            functools.partial(finish_kernel, group, half, slot_rows),
+            out_shape=(
+                jax.ShapeDtypeStruct((row_count, vocab), jnp.float32),
+                jax.ShapeDtypeStruct((8, LANES), jnp.float32),
+            ),
+            in_specs=[smem, smem, vmem, vmem, hbm, hbm],
+            out_specs=(vmem, vmem),
+            scratch_shapes=[
+                pltpu.VMEM((group, half, LANES), jnp.float32),
+                logit,
+                pltpu.VMEM((groups * COLS, LANES), jnp.float32),
+                pieces, pieces, dma((group // BATCH,)), dma,
+            ],
+            compiler_params=pltpu.CompilerParams(vmem_limit_bytes=VMEM_LIMIT),
+            name="finish",
+        )(rcols[:, slot_rows, :].reshape(-1), mix_weight, rcols, rstat, recv, logits)
 
         def dense(unused):
             me = lax.axis_index("model")

time: 309 us -> 245 us (0.79)
  the two profiles are of different devices: /device:TPU:55 before, /device:TPU:21 now
where the time goes in v3:
time: 245 us; the launch traced here: 243 us
  Pallas kernels  231 us (94%)
  other arithmetic  7.28 us (3%)
  local copies, waits for them, and re-layouts  2.73 us (1%)
    pallas_call x1, Pallas kernels, local_step(): pl.pallas_call(functools.partial(exchange_kernel, group, half, slot_rows)...  157 us
    pallas_call x1, Pallas kernels, local_step(): pl.pallas_call(functools.partial(finish_kernel, group, half, slot_rows),...  69.8 us
    sort x1, other arithmetic, local_step(): lax.sort((tok_shard, lax.iota(jnp.int32, n_local)), num_keys=1, is_stable...  7.28 us

profile of v3, /device:TPU:21, one launch (start us, length us, event | category | flops | bytes accessed | tf_op | source)
XLA Modules:
  0.0 243.3 jit_solution(17012376760432020967)
XLA Ops:
  0.0 7.3 %sort.15 = (s32[16384]{0:T(1024)S(1)}, s32[16384]{0:T(1024)S(1)}) sort(s32[16384]{0:T(1024)} %param.13, s32[16384]{0:T(1024)S(1)} %iota.3), dimensions={0}, to_apply=%region_0.0 | sort | flops 229376 | bytes 262144 | tf_op jit(solution)/shard_map/sort | solution.py:387
  7.3 0.7 pad_bitcast_fusion
  8.0 3.9 %slots.1 = (s32[16,11,128]{2,1,0:T(8,128)}, s32[160,128]{1,0:T(8,128)}, f32[8,128]{1,0:T(8,128)}) custom-call(s32[146,128]{1,0:T(8,128)} %get-tuple-element.241.tok_ref, s32[146,128]{1,0:T(8,128)} %get-tuple-element.240.ord_ref), custom_call_target="tpu_custom_call" | custom-call | tf_op jit(solution)/shard_map/slots/pallas_call | solution.py:400
  12.5 157.2 %exchange.1 = (f32[16,584,128]{2,1,0:T(8,128)}, s32[16,11,128]{2,1,0:T(8,128)}, f32[16,8,128]{2,1,0:T(8,128)}, f32[9496,128]{1,0:T(8,128)}) custom-call(s32[20480]{0:T(1024)} %bitcast.35, f32[1]{0:T(128)S(6)} %copy.35.temp_ref, bf16[64,1536]{1,0:T(8,128)(2,1)} %query_ref.1, f32[8,128]{1,0:T(8,128)} %get-tuple-element.174.over_ref, ...), custom_call_target="tpu_custom_call" | custom-call | tf_op jit(solution)/shard_map/exchange/pallas_call | solution.py:415
  169.7 1.4 slice.21
  171.8 0.0 copy-start.1
  171.8 69.8 %finish.1 = (f32[64,9496]{1,0:T(8,128)}, f32[8,128]{1,0:T(8,128)S(1)}) custom-call(s32[2048]{0:T(1024)} %bitcast.36, f32[1]{0:T(128)S(6)} %copy.36.mix_ref, s32[16,11,128]{2,1,0:T(8,128)} %get-tuple-element.176.rcol, f32[16,8,128]{2,1,0:T(8,128)} %get-tuple-element.177.stat, f32[16,584,128]{2,1,0:T(8,128)} %get-tuple-element.178.recv_hbm, ...), custom_call_target="tpu_custom_call" | custom-call | tf_op jit(solution)/shard_map/finish/pallas_call | solution.py:444
  241.6 0.6 slice.22
  242.9 0.0 copy-done.1
  242.9 0.2 conditional.1
  (1 shorter events, 0.0 us)
Async XLA Ops:
  171.8 71.1 %copy-start.1 = (bf16[64,1536]{1,0:T(8,128)(2,1)S(1)}, bf16[64,1536]{1,0:T(8,128)(2,1)}, u32[]{:S(2)}) copy-start(bf16[64,1536]{1,0:T(8,128)(2,1)} %query_ref.1) | copy-start | bytes 589828

commit v4 on v3

--- a/solution.py
+++ b/solution.py
@@ -14,9 +14,9 @@
 KEY_BUFS = 4
 HEAD_TILE = 512
 HEAD_BUFS = 3
-COLS = 256
-WINDOW = 64
-BATCH = 4
+HISTS = 8
+ROWS = 16
+CLEAR = 216
 VMEM_LIMIT = 60 * 1024 * 1024
 
 
@@ -27,15 +27,12 @@
 def slot_kernel(group, vocab, cap, rows, n_local, tok_ref, ord_ref, col_ref, idx_ref, over_ref):
     lane = lax.broadcasted_iota(jnp.int32, (rows, LANES), 1)
     slot = lax.broadcasted_iota(jnp.int32, (rows, LANES), 0) * LANES + lane
-    bound = lax.broadcasted_iota(jnp.int32, (LANES, LANES), 0)
-    across = lax.broadcasted_iota(jnp.int32, (LANES, LANES), 1)
     tokens = tok_ref[: n_local // LANES, :]
 
     def below(limit):
         return jnp.sum((tokens < limit).astype(jnp.int32))
 
     starts = [0] + [below(d * vocab) for d in range(1, group)] + [n_local]
-    table = jnp.zeros((LANES, LANES), jnp.float32)
     most = jnp.int32(0)
     for d in range(group):
         start, count = starts[d], starts[d + 1] - starts[d]
@@ -49,33 +46,23 @@
             return jnp.where(lane < LANES - off, low, high)
 
         used = slot < count
-        col = jnp.where(used, shifted(tok_ref) - d * vocab, vocab)
-        col_ref[d, :rows, :] = col
+        col_ref[d] = jnp.where(used, shifted(tok_ref) - d * vocab, vocab)
         idx_ref[d * rows : (d + 1) * rows, :] = jnp.where(used, shifted(ord_ref), 0)
-        first = jnp.where(used, col // COLS, LANES)
-        hits = jnp.zeros((LANES, LANES), jnp.float32)
-        for r in range(rows):
-            hits = hits + jnp.where(first[r : r + 1, :] < bound, 1.0, 0.0)
-        table = jnp.where(across == d, jnp.sum(hits, axis=1, keepdims=True), table)
-    widest = jnp.max(table[1:, :] - table[:-1, :])
-    over = jnp.where((most > cap) | (widest > WINDOW), 1.0, 0.0)
+    over = jnp.where(most > cap, 1.0, 0.0)
     over_ref[...] = jnp.full((8, LANES), over, jnp.float32)
-    turned = jnp.minimum(table, float(cap)).T.astype(jnp.int32)
-    for d in range(group):
-        col_ref[d, rows : rows + 1, :] = turned[d : d + 1, :]
 
 
 def exchange_kernel(
     group, half, rows, idx_ref, temp_ref, query_ref, over_ref, col_ref, key_hbm, head_hbm,
     recv_hbm, rcol_hbm, rstat_hbm, logit_hbm,
-    key_buf, head_buf, turned, score, send, relay, stat, logit,
-    key_sem, head_sem, data_send, data_recv, relay_send, relay_recv, col_send, col_recv,
+    key_buf, head_buf, turned, score, send, stat, logit,
+    key_sem, head_sem, data_send, data_recv, col_send, col_recv,
     stat_send, stat_recv, own_sem,
 ):
     me = lax.axis_index("model")
     n_local, vocab = key_hbm.shape[0], head_hbm.shape[0]
     slots = rows * LANES
-    mid, quarter = group // 2, group // 4
+    mid = group // 2
 
     def peer(k):
         return {"model": lax.rem(me + k, group)}
@@ -155,9 +142,6 @@
     def stat_copy(k):
         return remote(stat, rstat_hbm.at[k], stat_send.at[k], stat_recv.at[k], k)
 
-    first_leg = remote(send.at[mid], relay, relay_send, relay_recv, group - quarter)
-    second_leg = remote(relay, recv_hbm.at[mid], data_send.at[mid], data_recv.at[mid], group - quarter)
-
     def pack(k):
         base = lax.rem(me + k, group) * slots
 
@@ -170,7 +154,7 @@
                 send[k, pl.ds(j, 1), :] = row
             return carry
 
-        lax.fori_loop(0, half // 8, tile, 0)
+        lax.fori_loop(0, half // 8, tile, 0, unroll=2)
 
     for k in range(1, group):
         cols_copy(k).start()
@@ -182,11 +166,9 @@
         pack(k)
         if waiting is not None:
             waiting.start()
-        waiting = first_leg if k == mid else data_copy(k)
+        waiting = data_copy(k)
     pack(0)
     waiting.start()
-    first_leg.wait()
-    second_leg.start()
 
     def head_tile(tile, where):
         tile = jnp.dot(tile, turned[...], preferred_element_type=jnp.float32)
@@ -236,25 +218,21 @@
     for k in range(1, group):
         stat_copy(k).wait()
         cols_copy(k).wait()
-        if k == mid:
-            second_leg.wait()
-        else:
-            data_copy(k).wait()
+        data_copy(k).wait()
 
 
 def finish_kernel(
-    group, half, rows, off_smem, mix_ref, rcol, stat, recv_hbm, logit_hbm, out_ref, sum_ref,
-    recv, logit, hist, piece_a, piece_b, recv_sem, logit_sem,
+    group, half, slots, col_ref, mix_ref, stat, recv_hbm, logit_hbm, out_ref, sum_ref,
+    recv, logit, *rest_refs,
 ):
+    hists, (recv_sem, logit_sem) = rest_refs[:HISTS], rest_refs[HISTS:]
     vocab = logit_hbm.shape[0]
-    batches = group // BATCH
-
-    def fetch(b):
-        where = pl.ds(b * BATCH, BATCH)
-        return pltpu.make_async_copy(recv_hbm.at[where], recv.at[where], recv_sem.at[b])
-
-    for b in range(batches):
-        fetch(b).start()
+
+    def fetch(d):
+        return pltpu.make_async_copy(recv_hbm.at[d], recv.at[d], recv_sem.at[d])
+
+    for d in range(group):
+        fetch(d).start()
     fetch_logit = pltpu.make_async_copy(logit_hbm, logit, logit_sem)
     fetch_logit.start()
 
@@ -278,72 +256,39 @@
     sum_ref[3:4, :] = lm_sum
     sum_ref[4:8, :] = jnp.broadcast_to(over, (4, LANES))
 
-    hist[...] = jnp.zeros_like(hist)
-    for pieces in (piece_a, piece_b):
-        pieces[:, 2 * half :, :] = jnp.zeros((BATCH, WINDOW, LANES), jnp.float32)
-
-    lane = lax.broadcasted_iota(jnp.int32, (1, LANES), 1)
-    left = lane < LANES // 2
-    column = lax.broadcasted_iota(jnp.int32, (COLS, LANES), 0)
-
-    def split(i, start, count, value):
-        high = value.astype(jnp.bfloat16).astype(jnp.float32)
-        rest = value - high
-        middle = rest.astype(jnp.bfloat16).astype(jnp.float32)
-        piece_a[i, pl.ds(start, count), :] = jnp.where(left, high, middle)
-        piece_b[i, pl.ds(start, count), :] = rest - middle
-
-    def one_batch(b, carry):
-        fetch(b).wait()
-        for i in range(BATCH):
-
-            def unpack(t, carry):
-                start = pl.multiple_of(t * 8, 8)
-                value = jnp.exp(recv[b * BATCH + i, pl.ds(start, 8), :] - knn_max)
-                other = pltpu.roll(value, LANES // 2, 1)
-                split(i, start, 8, jnp.where(left, value, other))
-                split(i, pl.multiple_of(half + start, 8), 8, jnp.where(left, other, value))
-                return carry
-
-            lax.fori_loop(0, half // 8, unpack, 0, unroll=4)
-
-        def one_group(g, carry):
-            values, hots = [], []
-            pair = []
-            for i in range(BATCH):
-                k = b * BATCH + i
-                start = off_smem[k * LANES + g]
-                values.append(
-                    jnp.concatenate(
-                        [
-                            piece_a[i, pl.ds(start, WINDOW), :].astype(jnp.bfloat16),
-                            piece_b[i, pl.ds(start, WINDOW), :].astype(jnp.bfloat16),
-                        ],
-                        axis=1,
-                    )
-                )
-                row, off = start // LANES, start % LANES
-                low = rcol[k, pl.ds(row, 1), :]
-                high = rcol[k, pl.ds(jnp.minimum(row + 1, rows - 1), 1), :]
-                shift = (2 * LANES - off + WINDOW * (i % 2)) % LANES
-                seen = jnp.where(lane < off, high, low)
-                pair.append(pltpu.roll(seen, shift, 1))
-                if i % 2:
-                    cols = jnp.where(left, pair[i - 1], pair[i]) - g * COLS
-                    hots.append(jnp.where(column == cols, 1.0, 0.0).astype(jnp.bfloat16))
-            part = jnp.dot(
-                jnp.concatenate(hots, axis=1), jnp.concatenate(values, axis=0),
-                preferred_element_type=jnp.float32,
-            )
-            where = pl.ds(pl.multiple_of(g * COLS, COLS), COLS)
-            both = part[:, :LANES]
-            hist[where, :] += both + pltpu.roll(both, LANES // 2, 1) + part[:, LANES:]
+    def clear(i, carry):
+        where = pl.ds(pl.multiple_of(i * CLEAR, CLEAR), CLEAR)
+        for hist in hists:
+            hist[where, :] = jnp.zeros((CLEAR, LANES), jnp.float32)
+        return carry
+
+    lax.fori_loop(0, hists[0].shape[0] // CLEAR, clear, 0)
+
+    def one_source(d, carry):
+        fetch(d).wait()
+        recv[d] = jnp.exp(recv[d] - knn_max)
+
+        def add_rows(j, count):
+            base = d * slots + j
+            for i in range(count):
+                row = recv[d, pl.ds(j + i, 1), :]
+                low = hists[2 * (i % (HISTS // 2))]
+                high = hists[2 * (i % (HISTS // 2)) + 1]
+                a = col_ref[base + i]
+                low[pl.ds(a, 1), :] = low[pl.ds(a, 1), :] + row
+                b = col_ref[base + half + i]
+                high[pl.ds(b, 1), :] = high[pl.ds(b, 1), :] + row
+
+        def step(t, carry):
+            add_rows(t * ROWS, ROWS)
             return carry
 
-        lax.fori_loop(0, hist.shape[0] // COLS, one_group, 0, unroll=2)
+        lax.fori_loop(0, half // ROWS, step, 0)
+        if half % ROWS:
+            add_rows(half // ROWS * ROWS, half % ROWS)
         return carry
 
-    lax.fori_loop(0, batches, one_batch, 0)
+    lax.fori_loop(0, group, one_source, 0)
     fetch_logit.wait()
 
     mix = mix_ref[0]
@@ -352,7 +297,12 @@
 
     def tile(start, count):
         where = pl.ds(start, count)
-        prob = hist[where, :] * knn_scale + jnp.exp(logit[where, :] - lm_max) * lm_scale
+        low, high = hists[0][where, :], hists[1][where, :]
+        for hist in range(2, HISTS, 2):
+            low = low + hists[hist][where, :]
+            high = high + hists[hist + 1][where, :]
+        hist = low + pltpu.roll(high, LANES // 2, 1)
+        prob = hist * knn_scale + jnp.exp(logit[where, :] - lm_max) * lm_scale
         return jnp.log(prob)
 
     full = vocab // LANES
@@ -382,7 +332,6 @@
         half = cap // 2
         slot_rows = round_up(cap, LANES) // LANES
         slots = slot_rows * LANES
-        groups = round_up(vocab, 2 * COLS) // COLS
 
         order_tok, order_idx = lax.sort(
             (tok_shard, lax.iota(jnp.int32, n_local)), num_keys=1, is_stable=False
@@ -396,7 +345,7 @@
         smem = pl.BlockSpec(memory_space=pltpu.SMEM)
         vmem = pl.BlockSpec(memory_space=pltpu.VMEM)
         hbm = pl.BlockSpec(memory_space=pl.ANY)
-        table = jax.ShapeDtypeStruct((group, slot_rows + 1, LANES), jnp.int32)
+        table = jax.ShapeDtypeStruct((group, slot_rows, LANES), jnp.int32)
         cols, idx, over = pl.pallas_call(
             functools.partial(slot_kernel, group, vocab, cap, slot_rows, n_local),
             out_shape=(
@@ -410,7 +359,6 @@
         )(tok_2d, idx_2d)
 
         dma = pltpu.SemaphoreType.DMA
-        chunk = pltpu.VMEM((half, LANES), jnp.float32)
         logit = pltpu.VMEM((vocab, LANES), jnp.float32)
         recv, rcols, rstat, logits = pl.pallas_call(
             functools.partial(exchange_kernel, group, half, slot_rows),
@@ -428,10 +376,9 @@
                 pltpu.VMEM((depth, LANES), jnp.bfloat16),
                 pltpu.VMEM((n_local, LANES), jnp.float32),
                 pltpu.VMEM((group, half, LANES), jnp.float32),
-                chunk,
                 pltpu.VMEM((8, LANES), jnp.float32),
                 logit,
-                dma((KEY_BUFS,)), dma((HEAD_BUFS + 1,)), dma((group,)), dma((group,)), dma, dma,
+                dma((KEY_BUFS,)), dma((HEAD_BUFS + 1,)), dma((group,)), dma((group,)),
                 dma((group,)), dma((group,)), dma((group,)), dma((group,)), dma((4,)),
             ],
             compiler_params=pltpu.CompilerParams(
@@ -440,24 +387,23 @@
             name="exchange",
         )(idx.reshape(-1), temperature, queries, over, cols, key_shard, w_shard.T)
 
-        pieces = pltpu.VMEM((BATCH, 2 * half + WINDOW, LANES), jnp.float32)
         fast, sums = pl.pallas_call(
-            functools.partial(finish_kernel, group, half, slot_rows),
+            functools.partial(finish_kernel, group, half, slots),
             out_shape=(
                 jax.ShapeDtypeStruct((row_count, vocab), jnp.float32),
                 jax.ShapeDtypeStruct((8, LANES), jnp.float32),
             ),
-            in_specs=[smem, smem, vmem, vmem, hbm, hbm],
+            in_specs=[smem, smem, vmem, hbm, hbm],
             out_specs=(vmem, vmem),
             scratch_shapes=[
                 pltpu.VMEM((group, half, LANES), jnp.float32),
                 logit,
-                pltpu.VMEM((groups * COLS, LANES), jnp.float32),
-                pieces, pieces, dma((group // BATCH,)), dma,
+                *[pltpu.VMEM((round_up(vocab + 1, CLEAR), LANES), jnp.float32)] * HISTS,
+                dma((group,)), dma,
             ],
             compiler_params=pltpu.CompilerParams(vmem_limit_bytes=VMEM_LIMIT),
             name="finish",
-        )(rcols[:, slot_rows, :].reshape(-1), mix_weight, rcols, rstat, recv, logits)
+        )(rcols.reshape(-1), mix_weight, rstat, recv, logits)
 
         def dense(unused):
             me = lax.axis_index("model")

time: 245 us -> 201 us (0.82)
  Pallas kernels: 231 us -> 186 us
    pallas_call x1, Pallas kernels: 69.8 us -> 37.9 us  [local_step(): pl.pallas_call(functools.partial(finish_kernel, group, half, slots), out_...]
    pallas_call x1, Pallas kernels: 157 us -> 146 us  [local_step(): pl.pallas_call(functools.partial(exchange_kernel, group, half, slot_rows)...]
where the time goes in v4:
time: 201 us; the launch traced here: 199 us
  Pallas kernels  186 us (93%)
  other arithmetic  7.28 us (4%)
  local copies, waits for them, and re-layouts  2.83 us (1%)
  between operations  2.2 us (1%)
    pallas_call x1, Pallas kernels, local_step(): pl.pallas_call(functools.partial(exchange_kernel, group, half, slot_rows)...  146 us
    pallas_call x1, Pallas kernels, local_step(): pl.pallas_call(functools.partial(finish_kernel, group, half, slots), out_...  37.9 us
    sort x1, other arithmetic, local_step(): lax.sort((tok_shard, lax.iota(jnp.int32, n_local)), num_keys=1, is_stable...  7.28 us

profile of v4, /device:TPU:21, one launch (start us, length us, event | category | flops | bytes accessed | tf_op | source)
XLA Modules:
  0.0 198.6 jit_solution(17649828475646183613)
XLA Ops:
  0.0 7.3 %sort.15 = (s32[16384]{0:T(1024)S(1)}, s32[16384]{0:T(1024)S(1)}) sort(s32[16384]{0:T(1024)} %param.13, s32[16384]{0:T(1024)S(1)} %iota.3), dimensions={0}, to_apply=%region_0.0 | sort | flops 229376 | bytes 262144 | tf_op jit(solution)/shard_map/sort | solution.py:336
  7.3 0.7 pad_bitcast_fusion
  8.0 2.0 %slots.1 = (s32[16,10,128]{2,1,0:T(8,128)}, s32[160,128]{1,0:T(8,128)}, f32[8,128]{1,0:T(8,128)}) custom-call(s32[146,128]{1,0:T(8,128)} %get-tuple-element.241.tok_ref, s32[146,128]{1,0:T(8,128)} %get-tuple-element.240.ord_ref), custom_call_target="tpu_custom_call" | custom-call | tf_op jit(solution)/shard_map/slots/pallas_call | solution.py:349
  10.6 146.2 %exchange.1 = (f32[16,584,128]{2,1,0:T(8,128)}, s32[16,10,128]{2,1,0:T(8,128)}, f32[16,8,128]{2,1,0:T(8,128)}, f32[9496,128]{1,0:T(8,128)}) custom-call(s32[20480]{0:T(1024)} %bitcast.34, f32[1]{0:T(128)S(6)} %copy.35.temp_ref, bf16[64,1536]{1,0:T(8,128)(2,1)} %query_ref.1, f32[8,128]{1,0:T(8,128)} %get-tuple-element.174.over_ref, ...), custom_call_target="tpu_custom_call" | custom-call | tf_op jit(solution)/shard_map/exchange/pallas_call | solution.py:363
  156.9 1.5 reshape.57.col_ref
  159.1 0.0 copy-start.1
  159.1 37.9 %finish.1 = (f32[64,9496]{1,0:T(8,128)}, f32[8,128]{1,0:T(8,128)S(1)}) custom-call(s32[20480]{0:T(1024)} %reshape.57.col_ref, f32[1]{0:T(128)S(6)} %copy.36.mix_ref, f32[16,8,128]{2,1,0:T(8,128)} %get-tuple-element.177.stat, f32[16,584,128]{2,1,0:T(8,128)} %get-tuple-element.178.recv_hbm, f32[9496,128]{1,0:T(8,128)} %get-tuple-element.179.logit_hbm), custom_call_target="tpu_custom_call" | custom-call | tf_op jit(solution)/shard_map/finish/pallas_call | solution.py:390
  197.0 0.6 slice.18
  198.3 0.0 copy-done.1
  198.3 0.2 conditional.1
  (1 shorter events, 0.0 us)
Async XLA Ops:
  159.1 39.2 %copy-start.1 = (bf16[64,1536]{1,0:T(8,128)(2,1)S(1)}, bf16[64,1536]{1,0:T(8,128)(2,1)}, u32[]{:S(2)}) copy-start(bf16[64,1536]{1,0:T(8,128)(2,1)} %query_ref.1) | copy-start | bytes 589828
